TPU v7x, 32 devices: a whole 2x2x4 slice. The times are simulated.
32 devices in a mesh: dp: 1, ep: 32 (over x, y, z, core).
Axes of the slice: x: 2, y: 2, z: 4, core: 2. Of those that a mesh axis runs over, the one named last changes fastest.
Arguments:
- x: bfloat16 [1, 32, 256, 1792], P('dp', 'ep')
- expert: int32 [1, 32, 256, 8], P('dp', 'ep')
- slot: int32 [1, 32, 256, 8], P('dp', 'ep')
- gate: float32 [1, 32, 256, 8], P('dp', 'ep')
- w_gate: bfloat16 [96, 1792, 2048], P('ep')
- w_up: bfloat16 [96, 1792, 2048], P('ep')
- w_down: bfloat16 [96, 2048, 1792], P('ep')
- s_gate: bfloat16 [1792, 2048], replicated
- s_up: bfloat16 [1792, 2048], replicated
- s_down: bfloat16 [2048, 1792], replicated
Outputs:
- y: bfloat16 [1, 32, 256, 1792], P('dp', 'ep')
All inputs are finite; a program needn't handle non-finite values.
Results may differ from a plain program's by a relative error of at most 0.009.
Values are sent between devices in bfloat16 or wider.
A program may use at most 2 GiB of HBM per device.

v0:
```python
import jax
import jax.numpy as jnp
from jax import lax
from jax.sharding import NamedSharding, PartitionSpec as P


def einsum(form, a, b):
    return jnp.einsum(form, a.astype(jnp.float32), b.astype(jnp.float32))


def for_all(x, s_gate, s_up, s_down):
    h = jax.nn.silu(einsum("...d,df->...f", x, s_gate)) * einsum("...d,df->...f", x, s_up)
    return einsum("...f,fd->...d", h.astype(jnp.bfloat16), s_down)


def solution(mesh):
    def placed(v, *spec):
        return lax.with_sharding_constraint(v, NamedSharding(mesh, P(*spec)))

    def step(x, expert, slot, gate, w_gate, w_up, w_down, s_gate, s_up, s_down):
        experts, (tokens, top) = w_gate.shape[0], expert.shape[2:]
        slots = 5 * tokens * top // (4 * experts)
        to_expert = jax.nn.one_hot(expert, experts, dtype=jnp.bfloat16)
        to_slot = jax.nn.one_hot(slot, slots, dtype=jnp.bfloat16)
        weighted = to_expert * gate[..., None].astype(jnp.bfloat16)
        dispatch = einsum("abtke,abtkc->abtec", to_expert, to_slot).astype(jnp.bfloat16)
        combine = einsum("abtke,abtkc->abtec", weighted, to_slot).astype(jnp.bfloat16)
        z = einsum("abtec,abtd->aebcd", dispatch, x).astype(jnp.bfloat16)
        z = placed(z, "dp", None, "ep", None, None)
        z = placed(z, "dp", "ep", None, None, None)
        h = jax.nn.silu(einsum("aebcd,edf->aebcf", z, w_gate))
        h = (h * einsum("aebcd,edf->aebcf", z, w_up)).astype(jnp.bfloat16)
        out = einsum("aebcf,efd->aebcd", h, w_down).astype(jnp.bfloat16)
        out = placed(out, "dp", "ep", None, None, None)
        out = placed(out, "dp", None, "ep", None, None)
        y = einsum("abtec,aebcd->abtd", combine, out)
        return (y + for_all(x, s_gate, s_up, s_down)).astype(jnp.bfloat16)

    return step
```

profile of v0, /device:TPU:0, one launch (start us, length us, event | category | flops | bytes accessed | tf_op | source)
XLA Modules:
  0.0 676.2 jit_solution(486354043155288091)
XLA Ops:
  0.0 0.0 copy-start
  0.0 0.9 copy.11
  0.9 0.0 copy-start.1
  0.9 0.8 copy.13
  1.8 0.0 copy-start.3
  1.8 2.6 convolution_convert_fusion.1
  4.4 0.0 copy-done
  4.4 6.9 %convert_bitcast_fusion = bf16[1,96,1,26,1792]{4,1,3,2,0:T(8,128)(2,1)} fusion(bf16[256,96,26]{1,2,0:T(8,128)(2,1)S(1)} %convolution_convert_fusion.1, bf16[1,1,256,1792]{3,2,1,0:T(8,128)(2,1)S(1)} %copy-done), kind=kOutput, calls=%fused_computation.18 | convolution fusion | flops 2294562816 | bytes 11141120 | tf_op jit(solution)/abtec,abtd->aebcd/dot_general | solution.py:8
  11.3 12.9 %copy.15 = bf16[1,96,1,26,1792]{4,3,1,2,0:T(8,128)(2,1)} copy(bf16[1,96,1,26,1792]{4,1,3,2,0:T(8,128)(2,1)} %convert_bitcast_fusion) | data formatting | bytes 17891328 | tf_op jit(solution)/convert_element_type | solution.py:28
  24.2 0.0 copy-done.1
  24.2 0.0 copy-done.3
  24.2 254.0 %all-to-all.4 = bf16[1,32,3,1,26,1792]{5,4,2,3,0,1:T(8,128)(2,1)} all-to-all(bf16[1,32,3,1,26,1792]{5,4,2,3,0,1:T(8,128)(2,1)} %bitcast.132), channel_id=1, replica_groups=mesh['dp'=1,'ep'=32] {'ep'}, dimensions={1} | all-to-all | bytes 17891328 | tf_op jit(solution)/sharding_constraint;jit(solution)/sharding_constraint | solution.py:18
  278.2 48.9 %fusion.2 = f32[3,32,26,2048]{3,1,2,0:T(8,128)} fusion(bf16[3,1792,2048]{2,1,0:T(8,128)(2,1)} %param.5, bf16[1,32,3,1,26,1792]{5,4,2,3,0,1:T(8,128)(2,1)} %all-to-all.4), kind=kOutput, calls=%fused_computation.2 | convolution fusion | flops 18320719872 | bytes 51412992 | tf_op jit(solution)/aebcd,edf->aebcf/dot_general | solution.py:8
  327.0 34.7 %fusion.6 = bf16[1,3,32,26,2048]{4,2,3,1,0:T(8,128)(2,1)} fusion(f32[3,32,26,2048]{3,1,2,0:T(8,128)} %fusion.2, bf16[3,1792,2048]{2,1,0:T(8,128)(2,1)} %param.4, bf16[1,32,3,1,26,1792]{5,4,2,3,0,1:T(8,128)(2,1)} %all-to-all.4), kind=kOutput, calls=%fused_computation.7 | convolution fusion | flops 18351390720 | bytes 61636608 | tf_op jit(solution)/aebcd,edf->aebcf/dot_general | solution.py:8
  361.8 28.9 %convert_bitcast_fusion.1 = bf16[1,3,32,1,26,1792]{5,2,4,1,3,0:T(8,128)(2,1)} fusion(bf16[3,2048,1792]{2,1,0:T(8,128)(2,1)} %param.6, bf16[1,3,32,26,2048]{4,2,3,1,0:T(8,128)(2,1)} %fusion.6), kind=kOutput, calls=%fused_computation.19 | convolution fusion | flops 18325192704 | bytes 41189376 | tf_op jit(solution)/aebcf,efd->aebcd/dot_general | solution.py:8
  390.7 12.9 %copy.18 = bf16[1,3,32,1,26,1792]{5,4,1,3,0,2:T(8,128)(2,1)} copy(bf16[1,3,32,1,26,1792]{5,2,4,1,3,0:T(8,128)(2,1)} %convert_bitcast_fusion.1) | data formatting | bytes 17891328 | tf_op jit(solution)/sharding_constraint;jit(solution)/sharding_constraint | solution.py:18
  403.6 0.0 copy-start.5
  403.6 0.0 copy-start.2
  403.6 0.0 copy-start.4
  403.6 3.9 all-to-all-start.1
  407.5 0.0 copy-done.5
  407.5 0.1 copy.12
  407.6 0.0 copy-done.2
  407.6 0.0 copy-done.4
  407.6 3.0 convolution_convert_fusion
  410.6 6.5 convolution_bitcast_fusion.1
  417.1 11.3 %fusion.50 = f32[256,1792]{1,0:T(8,128)} fusion(bf16[2048,1792]{1,0:T(8,128)(2,1)} %param.9, bf16[1792,2048]{1,0:T(8,128)(2,1)} %param.8, f32[1,256,2048]{2,1,0:T(8,128)} %convolution_bitcast_fusion.1, bf16[1,1,256,1792]{3,2,1,0:T(8,128)(2,1)S(1)} %copy-done), kind=kOutput, calls=%fused_computation.43 | convolution fusion | flops 3761242112 | bytes 19529728 | tf_op jit(solution)/...f,fd->...d/dot_general | solution.py:8
  428.4 220.9 %all-to-all-done.1 = bf16[1,3,32,1,26,1792]{5,4,1,3,0,2:T(8,128)(2,1)} async-done(((bf16[1,3,32,1,26,1792]{5,4,1,3,0,2:T(8,128)(2,1)}), bf16[1,3,32,1,26,1792]{5,4,1,3,0,2:T(8,128)(2,1)}, u32[]{:S(2)}, u32[]{:S(2)}) %all-to-all-start.1) | async-done | bytes 8945696 | tf_op jit(solution)/sharding_constraint;jit(solution)/sharding_constraint | solution.py:18
  649.2 26.5 %fusion.35 = bf16[1,1,256,1792]{3,2,1,0:T(8,128)(2,1)} fusion(f32[256,1792]{1,0:T(8,128)} %fusion.50, bf16[96,26,1792]{2,1,0:T(8,128)(2,1)} %bitcast.37, bf16[256,96,26]{1,2,0:T(8,128)(2,1)S(1)} %convolution_convert_fusion), kind=kOutput, calls=%fused_computation.30 | convolution fusion | flops 2291007488 | bytes 12976128 | tf_op jit(solution)/abtec,aebcd->abtd/dot_general | solution.py:8
  (1 shorter events, 0.0 us)
Async XLA Ops:
  0.0 4.4 copy-start
  0.9 23.3 %copy-start.1 = (s32[256,8]{1,0:T(8,128)}, s32[256,8]{1,0:T(8,128)S(1)}, u32[]{:S(2)}) copy-start(s32[256,8]{1,0:T(8,128)S(1)} %copy.11) | copy-start | bytes 24580
  1.8 22.4 %copy-start.3 = (s32[256,8]{1,0:T(8,128)}, s32[256,8]{1,0:T(8,128)S(1)}, u32[]{:S(2)}) copy-start(s32[256,8]{1,0:T(8,128)S(1)} %copy.13) | copy-start | bytes 24580
  403.6 3.9 copy-start.5
  403.6 4.0 copy-start.2
  403.6 4.0 copy-start.4
  403.6 245.7 %all-to-all-start.1 = ((bf16[1,3,32,1,26,1792]{5,4,1,3,0,2:T(8,128)(2,1)}), bf16[1,3,32,1,26,1792]{5,4,1,3,0,2:T(8,128)(2,1)}, u32[]{:S(2)}, u32[]{:S(2)}) async-start(bf16[1,3,32,1,26,1792]{5,4,1,3,0,2:T(8,128)(2,1)} %copy.18), calls=%async_computation.1 | async-start | bytes 22020096 | tf_op jit(solution)/sharding_constraint;jit(solution)/sharding_constraint | solution.py:18
where the time goes:
time: 683 us; the launch traced here: 676 us
  blocking collectives  254 us (37%)
  waiting for transfers between devices  221 us (32%)
  matrix products  169 us (25%)
  local copies, waits for them, and re-layouts  27.7 us (4%)
    another operation x1, blocking collectives, placed(): return lax.with_sharding_constraint(v, NamedSharding(mesh, P(*spec)))  254 us
    another operation x1, waiting for transfers between devices, placed(): return lax.with_sharding_constraint(v, NamedSharding(mesh, P(*spec)))  221 us
    dot_general x9, matrix products, einsum(): return jnp.einsum(form, a.astype(jnp.float32), b.astype(jnp.float32))  169 us
  transfers between devices with their start and end apart: 1, of which 1 were waited for; matrix products, arithmetic and copies ran while one was open for 3% of the time, Pallas kernels for 0%

commit v1 on v0

v1 whole, which is shorter than its diff:
```python
import jax
import jax.numpy as jnp
from jax import lax
from jax.sharding import PartitionSpec as P

F32, BF16 = jnp.float32, jnp.bfloat16


def dot(form, a, b):
    return jnp.einsum(form, a, b, preferred_element_type=F32)


def solution(mesh):
    def step(x, expert, slot, gate, w_gate, w_up, w_down, s_gate, s_up, s_down):
        tokens, top = expert.shape[2:]
        members = mesh.shape["ep"]
        own = w_gate.shape[0]
        slots = 5 * tokens * top // (4 * own * members)
        x0 = x[0, 0]
        table = jnp.concatenate(
            [
                expert[0, 0].astype(BF16),
                jnp.minimum(slot[0, 0], slots).astype(BF16),
                gate[0, 0].astype(BF16),
            ],
            axis=1,
        ).T
        xs = lax.all_gather(x0, "ep")
        ts = lax.all_gather(table, "ep")
        first = lax.axis_index("ep") * own
        e = ts[:, :top].astype(jnp.int32) - first
        c = ts[:, top : 2 * top].astype(jnp.int32)
        g = ts[:, 2 * top :]
        rows = own * slots
        pos = jnp.where((e >= 0) & (e < own) & (c < slots), e * slots + c, rows)
        hit = pos[:, :, None, :] == lax.broadcasted_iota(jnp.int32, (1, 1, rows, 1), 2)
        pick = jnp.any(hit, axis=1).astype(BF16)
        weigh = jnp.sum(jnp.where(hit, g[:, :, None, :].astype(F32), 0.0), axis=1).astype(BF16)
        z = dot("spt,std->spd", pick, xs).astype(BF16)
        z = z.reshape(members, own, slots, -1).transpose(1, 0, 2, 3).reshape(own, members * slots, -1)
        h = jax.nn.silu(dot("emd,edf->emf", z, w_gate)) * dot("emd,edf->emf", z, w_up)
        out = dot("emf,efd->emd", h.astype(BF16), w_down).astype(BF16)
        out = out.reshape(own, members, slots, -1).transpose(1, 0, 2, 3).reshape(members, rows, -1)
        part = dot("spt,spd->std", weigh, out).astype(BF16)
        y = lax.psum_scatter(part, "ep", scatter_dimension=0, tiled=False)
        h = jax.nn.silu(dot("td,df->tf", x0, s_gate)) * dot("td,df->tf", x0, s_up)
        shared = dot("tf,fd->td", h.astype(BF16), s_down)
        return (y.astype(F32) + shared).astype(BF16)[None, None]

    row = P("dp", "ep", None, None)
    w = P("ep", None, None)
    s = P(None, None)
    return jax.shard_map(
        step, mesh=mesh, in_specs=(row, row, row, row, w, w, w, s, s, s), out_specs=row, check_vma=False
    )
```

time: 683 us -> 709 us (1.038)
  blocking collectives: 254 us -> 46.6 us
  waiting for transfers between devices: 221 us -> 426 us
  matrix products: 169 us -> 132 us
  local copies, waits for them, and re-layouts: 27.7 us -> 61.8 us
  other arithmetic: 0.01 us -> 19.3 us
  between operations: 0.55 us -> 13.7 us
    reduce_scatter x0 -> x1, waiting for transfers between devices: none -> 310 us  [step(): y = lax.psum_scatter(part, 'ep', scatter_dimension=0, tiled=False)]
    another operation x1 -> x0, blocking collectives: 254 us -> none  [placed(): return lax.with_sharding_constraint(v, NamedSharding(mesh, P(*spec)))]
    another operation x1 -> x0, waiting for transfers between devices: 221 us -> none  [placed(): return lax.with_sharding_constraint(v, NamedSharding(mesh, P(*spec)))]
    all_gather x0 -> x1, waiting for transfers between devices: none -> 116 us  [step(): xs = lax.all_gather(x0, 'ep')]
    all_gather x0 -> x1, blocking collectives: none -> 46.6 us  [step(): ts = lax.all_gather(table, 'ep')]
    dot_general x9 -> x6, matrix products: 169 us -> 132 us  [dot(): return jnp.einsum(form, a, b, preferred_element_type=F32)]
    transpose x0 -> x2, local copies, waits for them, and re-layouts: none -> 25.6 us  [the longest x1 12.9 us: step(): z.reshape(members, own, slots, -1).transpose(1, 0, 2, 3)]
    reshape x0 -> x2, local copies, waits for them, and re-layouts: none -> 25.1 us  [the longest x1 12.6 us: step(): out.reshape(own, members, slots, -1).transpose(1, 0, 2, 3)]
  transfers between devices with their start and end apart: 1 -> 2, of which waited for: 1 -> 2; matrix products, arithmetic and copies ran while one was open for 3% -> 3% of each run, Pallas kernels for 0% -> 0%
where the time goes in v1:
time: 709 us; the launch traced here: 700 us
  waiting for transfers between devices  426 us (60%)
  matrix products  132 us (19%)
  local copies, waits for them, and re-layouts  61.8 us (9%)
  blocking collectives  46.6 us (7%)
  other arithmetic  19.3 us (3%)
  between operations  13.7 us (2%)
    reduce_scatter x1, waiting for transfers between devices, step(): y = lax.psum_scatter(part, 'ep', scatter_dimension=0, tiled=False)  310 us
    dot_general x6, matrix products, dot(): return jnp.einsum(form, a, b, preferred_element_type=F32)  132 us
    all_gather x1, waiting for transfers between devices, step(): xs = lax.all_gather(x0, 'ep')  116 us
    all_gather x1, blocking collectives, step(): ts = lax.all_gather(table, 'ep')  46.6 us
  transfers between devices with their start and end apart: 2, of which 2 were waited for; matrix products, arithmetic and copies ran while one was open for 3% of the time, Pallas kernels for 0%

profile of v1, /device:TPU:0, one launch (start us, length us, event | category | flops | bytes accessed | tf_op | source)
XLA Modules:
  0.0 699.9 jit_solution(1283331826383178644)
XLA Ops:
  6.5 0.0 all-gather.4.cloned.1.call-start
  6.5 0.7 all-gather.4.cloned.1.call-update
  7.3 0.0 reduce-scatter.2.cloned.1.call-start
  7.3 0.7 convert_bitcast_fusion
  8.0 0.7 fusion.25
  8.7 46.6 %all-gather = bf16[768,256]{1,0:T(8,128)(2,1)S(1)} all-gather(bf16[24,256]{1,0:T(8,128)(2,1)S(1)} %maximum_bitcast_fusion), channel_id=2, replica_groups=mesh['dp'=1,'ep'=32] {'ep'}, dimensions={0}, use_global_device_ids=true | all-gather | bytes 405504 | tf_op jit(solution)/shard_map/all_gather | solution.py:29
  55.4 0.1 fusion.20
  55.5 9.0 %fusion.2 = pred[32,78,256]{2,1,0:T(8,128)(4,1)S(1)} fusion(s32[32,8,256]{2,1,0:T(8,128)S(1)} %fusion.20), kind=kLoop, calls=%fused_computation.6 | loop fusion | flops 9584640 | bytes 901120 | tf_op jit(solution)/shard_map/reduce_or | solution.py:37
  64.5 8.7 %select_reduce_fusion = bf16[32,78,256]{2,1,0:T(8,128)(2,1)} fusion(f32[32,8,256]{2,1,0:T(8,128)S(1)} %slice_convert_fusion, s32[32,8,256]{2,1,0:T(8,128)S(1)} %fusion.20), kind=kLoop, calls=%fused_computation.4 | loop fusion | flops 14696448 | bytes 1802240 | tf_op jit(solution)/shard_map/reduce_sum | solution.py:38
  73.2 115.6 %all-gather.4.cloned.1.call-done = bf16[32,1,256,1792]{3,2,1,0:T(8,128)(2,1)} async-done(((bf16[1,1,256,1792]{3,2,1,0:T(8,128)(2,1)}), bf16[32,1,256,1792]{3,2,1,0:T(8,128)(2,1)}) %all-gather.4.cloned.1.call-update) | async-done | bytes 29360144 | tf_op jit(solution)/shard_map/all_gather | solution.py:28
  188.8 15.5 %fusion.7 = bf16[32,78,1792]{2,1,0:T(8,128)(2,1)} fusion(pred[32,78,256]{2,1,0:T(8,128)(4,1)S(1)} %fusion.2, bf16[32,1,256,1792]{3,2,1,0:T(8,128)(2,1)} %all-gather.4.cloned.1.call-done), kind=kOutput, calls=%fused_computation.10 | convolution fusion | flops 2294562816 | bytes 38944768 | tf_op jit(solution)/shard_map/spt,std->spd/dot_general | solution.py:10
  204.4 10.0 %copy.23 = bf16[32,78,1792]{2,0,1:T(8,128)(2,1)} copy(bf16[32,78,1792]{2,1,0:T(8,128)(2,1)} %fusion.7) | data formatting | bytes 17891328 | tf_op jit(solution)/shard_map/convert_element_type | solution.py:39
  214.3 12.9 %copy.24 = bf16[3,32,26,1792]{3,2,1,0:T(8,128)(2,1)} copy(bf16[3,32,26,1792]{3,1,2,0:T(8,128)(2,1)} %bitcast.48) | data formatting | bytes 17891328 | tf_op jit(solution)/shard_map/transpose | solution.py:40
  227.2 12.5 %reshape.23 = bf16[3,832,1792]{2,1,0:T(8,128)(2,1)} reshape(bf16[3,32,26,1792]{3,2,1,0:T(8,128)(2,1)} %copy.24) | data formatting | bytes 17891328 | tf_op jit(solution)/shard_map/reshape | solution.py:40
  239.7 26.7 %fusion.28 = f32[3,832,2048]{2,1,0:T(8,128)} fusion(bf16[3,832,1792]{2,1,0:T(8,128)(2,1)} %reshape.23, bf16[3,1792,2048]{2,1,0:T(8,128)(2,1)} %param.14), kind=kOutput, calls=%fused_computation.37 | convolution fusion | flops 18320719872 | bytes 51412992 | tf_op jit(solution)/shard_map/emd,edf->emf/dot_general | solution.py:10
  266.4 48.1 %fusion.10 = bf16[3,832,1792]{2,1,0:T(8,128)(2,1)} fusion(bf16[3,2048,1792]{2,1,0:T(8,128)(2,1)} %param.16, f32[3,832,2048]{2,1,0:T(8,128)} %fusion.28, bf16[3,832,1792]{2,1,0:T(8,128)(2,1)} %reshape.23, bf16[3,1792,2048]{2,1,0:T(8,128)(2,1)} %param.15), kind=kOutput, calls=%fused_computation.11 | convolution fusion | flops 36676583424 | bytes 82378752 | tf_op jit(solution)/shard_map/emf,efd->emd/dot_general | solution.py:10
  314.5 12.6 %reshape.24 = bf16[3,32,26,1792]{3,2,1,0:T(8,128)(2,1)} reshape(bf16[3,832,1792]{2,1,0:T(8,128)(2,1)} %fusion.10) | data formatting | bytes 17891328 | tf_op jit(solution)/shard_map/reshape | solution.py:43
  327.1 0.0 copy-start
  327.1 12.7 %copy.25 = bf16[32,3,26,1792]{3,0,2,1:T(8,128)(2,1)} copy(bf16[32,3,26,1792]{3,2,0,1:T(8,128)(2,1)} %bitcast.46) | data formatting | bytes 17891328 | tf_op jit(solution)/shard_map/transpose | solution.py:43
  339.8 0.0 copy-done
  339.8 26.7 %convolution_convert_fusion = bf16[32,256,1792]{2,1,0:T(8,128)(2,1)} fusion(bf16[32,78,1792]{2,0,1:T(8,128)(2,1)} %bitcast.47, bf16[32,78,256]{2,1,0:T(8,128)(2,1)S(1)} %copy-done), kind=kOutput, calls=%fused_computation.2 | convolution fusion | flops 2304770048 | bytes 39583744 | tf_op jit(solution)/shard_map/spt,spd->std/dot_general | solution.py:10
  366.5 0.0 copy-start.1
  366.5 0.0 reduce-scatter.2.cloned.1.call-update
  366.5 1.1 copy-done.1
  367.7 5.1 fusion.16
  372.8 309.7 %reduce-scatter.2.cloned.1.call-done = bf16[1,256,1792]{2,1,0:T(8,128)(2,1)} async-done(((bf16[32,256,1792]{2,1,0:T(8,128)(2,1)}), bf16[1,256,1792]{2,1,0:T(8,128)(2,1)}) %reduce-scatter.2.cloned.1.call-update) | async-done | bytes 917520 | tf_op jit(solution)/shard_map/reduce_scatter | solution.py:45
  682.5 10.4 %fusion.13 = bf16[1,1,256,1792]{3,2,1,0:T(8,128)(2,1)} fusion(bf16[2048,1792]{1,0:T(8,128)(2,1)} %param.19, bf16[1,256,1792]{2,1,0:T(8,128)(2,1)} %reduce-scatter.2.cloned.1.call-done, bf16[1792,2048]{1,0:T(8,128)(2,1)} %param.18, f32[256,2048]{1,0:T(8,128)S(1)} %fusion.16, bf16[1,1,256,1792]{3,2,1,0:T(8,128)(2,1)S(1)} %copy-done.1), kind=kOutput, calls=%fused_computation.16 | convolution fusion | flops 3762618368 | bytes 19529728 | tf_op jit(solution)/shard_map/tf,fd->td/dot_general | solution.py:10
  (2 shorter events, 0.0 us)
Async XLA Ops:
  6.5 182.3 %all-gather.4.cloned.1.call-start = ((), (), s32[]{:S(2)}) async-start(), calls=%async_computation.2 | async-start | bytes 30277632 | tf_op jit(solution)/shard_map/all_gather | solution.py:28
  7.3 675.2 %reduce-scatter.2.cloned.1.call-start = ((), (), s32[]{:S(2)}) async-start(), calls=%async_computation.1 | async-start | bytes 30277632 | tf_op jit(solution)/shard_map/reduce_scatter | solution.py:45
  327.1 12.7 %copy-start = (bf16[32,78,256]{2,1,0:T(8,128)(2,1)S(1)}, bf16[32,78,256]{2,1,0:T(8,128)(2,1)}, u32[]{:S(2)}) copy-start(bf16[32,78,256]{2,1,0:T(8,128)(2,1)} %select_reduce_fusion) | copy-start | bytes 3833860
  366.5 1.2 copy-start.1
Sparse Core Ops, SparseCore 0:
  10.2 178.5 all-gather.3
  366.6 315.8 reduce-scatter.1

commit v2 on v1

v2 whole, which is shorter than its diff:
```python
import functools

import jax
import jax.numpy as jnp
from jax import lax
from jax.experimental import pallas as pl
from jax.experimental.pallas import tpu as pltpu
from jax.sharding import PartitionSpec as P

F32, BF16, I32 = jnp.float32, jnp.bfloat16, jnp.int32
MESH = pl.DeviceIdType.MESH

SLOTS = 26
PLANE = 8
LINE = 4
OWN = 3
BLOCKS = OWN * PLANE
PAD = 32
START = (0, 24, 48, 72)
ROWS = (24, 24, 24, 32)
BACK = ((0, 0, 24), (1, 0, 24), (2, 0, 24), (3, 0, 16), (3, 16, 16))
HALF = 16
COLS = 256
WIDE = 512
DEEP_F, DEEP_D = 3, 4
CALLS = 1 + LINE * OWN


def loop(n, body):
    lax.fori_loop(0, n, lambda i, c: (body(i), c)[1], 0)


def kernel(
    x, tab, w_gate, w_up, w_down, s_gate, s_up, s_down, y,
    lines, tabs, staged, slots, back, terms, shared, hidden, pick, pick_next, fbuf, dbuf,
    z_send, z_recv, d_send, d_recv, r_send, r_recv, p_send, p_recv, f_sem, d_sem,
):
    me = lax.axis_index("ep")
    mx, my, mz, mc = me // 16, (me // 8) % 2, (me // 2) % 4, me % 2
    place = (me // 8) * 2 + mc
    depth = x.shape[1]
    nf, nd = s_gate.shape[1] // WIDE, depth // COLS

    def peer(j):
        px, py, pc = (mx + j // 4) % 2, (my + (j // 2) % 2) % 2, (mc + j % 2) % 2
        return {"ep": ((px * 2 + py) * 4 + mz) * 2 + pc}, (px * 2 + py) * 2 + pc

    def line_peer(o):
        pz = (mz + 1 - 2 * (mz % 2), (mz + 2) % 4, 3 - mz)[o - 1]
        return {"ep": ((mx * 2 + my) * 4 + pz) * 2 + mc}

    def wide(ref, i):
        return ref.at[:, pl.ds(pl.multiple_of(i * WIDE, WIDE), WIDE)]

    def narrow(ref, i):
        return ref.at[:, pl.ds(pl.multiple_of(i * COLS, COLS), COLS)]

    def f_copies(gate, up, i, s):
        return [
            pltpu.make_async_copy(wide(gate, i), fbuf.at[s, 0], f_sem.at[s, 0]),
            pltpu.make_async_copy(wide(up, i), fbuf.at[s, 1], f_sem.at[s, 1]),
        ]

    def start_f(g):
        n, i, s = g // nf, g % nf, g % DEEP_F

        @pl.when(n == 0)
        def _():
            for c in f_copies(s_gate, s_up, i, s):
                c.start()

        @pl.when((n > 0) & (n < CALLS))
        def _():
            e = (n + OWN - 1) % OWN
            for c in f_copies(w_gate.at[e], w_up.at[e], i, s):
                c.start()

    def start_d(g):
        n, i, s = g // nd, g % nd, g % DEEP_D

        @pl.when(n == 0)
        def _():
            pltpu.make_async_copy(narrow(s_down, i), dbuf.at[s], d_sem.at[s]).start()

        @pl.when((n > 0) & (n < CALLS))
        def _():
            e = (n + OWN - 1) % OWN
            pltpu.make_async_copy(narrow(w_down.at[e], i), dbuf.at[s], d_sem.at[s]).start()

    loop(DEEP_F, start_f)
    loop(DEEP_D, start_d)

    barrier = pltpu.get_barrier_semaphore()
    for o in range(1, LINE):
        pl.semaphore_signal(barrier, inc=1, device_id=line_peer(o), device_id_type=MESH)
    for j in range(1, PLANE):
        pl.semaphore_signal(barrier, inc=1, device_id=peer(j)[0], device_id_type=MESH)
    pl.semaphore_wait(barrier, LINE - 1 + PLANE - 1)

    def line_copies(o):
        return [
            pltpu.make_async_remote_copy(
                src_ref=src, dst_ref=dst.at[o - 1], send_sem=z_send.at[o - 1, i], recv_sem=z_recv.at[o - 1, i],
                device_id=line_peer(o), device_id_type=MESH,
            )
            for i, (src, dst) in enumerate(((tab, tabs), (x, lines)))
        ]

    for o in range(1, LINE):
        for c in line_copies(o):
            c.start()

    def build(ref, height, o, start, rows, weigh):
        table = tab if o == 0 else tabs.at[o - 1]
        code = table[0:8, :].astype(I32) - mz * 1024
        gates = table[8:16, :]
        r = lax.broadcasted_iota(I32, (height, code.shape[1]), 0)
        v = r + (start - SLOTS * o)
        ok = (v >= 0) & (v < SLOTS) & (r < rows)

        def block(b):
            want = jnp.where(ok, v + b * SLOTS, -7)
            acc = jnp.zeros(want.shape, F32)
            for i in range(8):
                value = gates[i : i + 1, :] if weigh else jnp.float32(1)
                acc = jnp.where(want == code[i : i + 1, :], value, acc)
            ref[pl.ds(pl.multiple_of(b * height, height), height), :] = acc.astype(BF16)

        loop(BLOCKS, block)

    def tokens_of(o):
        return x if o == 0 else lines.at[o - 1]

    def slot_copy(k, j):
        device, there = peer(j)
        return pltpu.make_async_remote_copy(
            src_ref=staged.at[k, :, there, 0 : ROWS[k]], dst_ref=slots.at[k, :, place, 0 : ROWS[k]],
            send_sem=d_send.at[k, j], recv_sem=d_recv.at[k, j], device_id=device, device_id_type=MESH,
        )

    def dispatch(k):
        if k:
            for c in line_copies(k):
                c.wait_recv()
        build(pick.at[0], PAD, k, START[k], ROWS[k], False)
        if k:
            build(pick.at[1], PAD, k - 1, START[k], ROWS[k], False)

        def columns(i):
            c = pl.ds(pl.multiple_of(i * COLS, COLS), COLS)
            out = jnp.dot(pick[0], tokens_of(k)[:, c], preferred_element_type=F32)
            if k:
                out += jnp.dot(pick[1], tokens_of(k - 1)[:, c], preferred_element_type=F32)
            staged[k, :, :, :, c] = out.astype(BF16).reshape(OWN, PLANE, PAD, COLS)

        loop(nd, columns)
        loop(PLANE - 1, lambda i: slot_copy(k, PLANE - 1 - i).start())
        slots[k, :, place] = staged[k, :, place]

    def ffn(n, read, write):
        def up(i):
            g = n * nf + i
            s = g % DEEP_F
            for c in f_copies(s_gate, s_up, 0, s):
                c.wait()
            z = read()
            a = jnp.dot(z, fbuf[s, 0], preferred_element_type=F32)
            b = jnp.dot(z, fbuf[s, 1], preferred_element_type=F32)
            hidden[:, pl.ds(pl.multiple_of(i * WIDE, WIDE), WIDE)] = (a * jax.nn.sigmoid(a) * b).astype(BF16)
            start_f(g + DEEP_F)

        def down(i):
            g = n * nd + i
            s = g % DEEP_D
            pltpu.make_async_copy(narrow(s_down, 0), dbuf.at[s], d_sem.at[s]).wait()
            write(
                pl.ds(pl.multiple_of(i * COLS, COLS), COLS),
                jnp.dot(hidden[...], dbuf[s], preferred_element_type=F32),
            )
            start_d(g + DEEP_D)

        loop(nf, up)
        loop(nd, down)

    def back_copy(p, j):
        k, r, rows = BACK[p]
        device, there = peer(j)
        return pltpu.make_async_remote_copy(
            src_ref=staged.at[k, :, there, r : r + rows], dst_ref=back.at[k, :, place, r : r + rows],
            send_sem=r_send.at[p, j], recv_sem=r_recv.at[p, j], device_id=device, device_id_type=MESH,
        )

    def send_back(p):
        loop(PLANE - 1, lambda i: back_copy(p, PLANE - 1 - i).start())
        k, r, rows = BACK[p]
        back[k, :, place, r : r + rows] = staged[k, :, place, r : r + rows]

    def term_copy(o):
        return pltpu.make_async_remote_copy(
            src_ref=lines.at[o - 1], dst_ref=terms.at[o - 1], send_sem=p_send.at[o - 1], recv_sem=p_recv.at[o - 1],
            device_id=line_peer(o), device_id_type=MESH,
        )

    for k in range(LINE - 1):
        back[k, :, :, ROWS[k] : PAD] = jnp.zeros((OWN, PLANE, PAD - ROWS[k], depth), BF16)

    dispatch(0)

    def write_shared(c, value):
        shared[:, c] = value

    ffn(0, lambda: x[...], write_shared)
    dispatch(1)

    def call(m):
        n = m + 1
        k, e = m // OWN, m % OWN
        for kk in range(LINE):
            @pl.when(m == kk * OWN)
            def _():
                def wait(i):
                    c = slot_copy(kk, i + 1)
                    c.wait_recv()
                    c.wait_send()

                loop(PLANE - 1, wait)

        def write(c, value):
            staged[k, e, :, :, c] = value.astype(BF16).reshape(PLANE, PAD, COLS)

        ffn(n, lambda: slots[k, e].reshape(PLANE * PAD, depth), write)

        @pl.when(m == 1)
        def _():
            dispatch(2)

        @pl.when(m == 5)
        def _():
            dispatch(3)

        @pl.when(m == 8)
        def _():
            send_back(2)

    loop(LINE * OWN, call)
    for p in (3, 4, 1, 0):
        send_back(p)

    def combine(o, pieces, write):
        for p in pieces:
            loop(PLANE - 1, lambda i: back_copy(p, i + 1).wait_recv())
        build(pick.at[0], PAD, o, START[o], ROWS[o], True)
        if o < LINE - 1:
            build(pick_next, HALF, o, START[o + 1], HALF, True)

        def columns(i):
            c = pl.ds(pl.multiple_of(i * COLS, COLS), COLS)

            def dot(weights, rows):
                return lax.dot_general(weights, rows, (((0,), (0,)), ((), ())), preferred_element_type=F32)

            out = dot(pick[0], back[o, :, :, :, c].reshape(BLOCKS * PAD, COLS))
            if o < LINE - 1:
                out += dot(pick_next[...], back[o + 1, :, :, 0:HALF, c].reshape(BLOCKS * HALF, COLS))
            write(c, out)

        loop(nd, columns)

    def keep(o):
        def write(c, value):
            lines[o - 1, :, c] = value.astype(BF16)

        return write

    for o, pieces in ((2, (2, 3)), (3, (4,)), (1, (1,))):
        for c in line_copies(o):
            c.wait_send()
        combine(o, pieces, keep(o))
        term_copy(o).start()

    def finish(c, value):
        for o in range(1, LINE):
            value += terms[o - 1, :, c].astype(F32)
        y[:, c] = (value + shared[:, c]).astype(BF16)

    loop(PLANE - 1, lambda i: back_copy(0, i + 1).wait_recv())
    for o in range(1, LINE):
        term_copy(o).wait()
    combine(0, (), finish)
    for p in range(len(BACK)):
        loop(PLANE - 1, lambda i: back_copy(p, i + 1).wait_send())


def solution(mesh):
    def step(x, expert, slot, gate, w_gate, w_up, w_down, s_gate, s_up, s_down):
        tokens, depth = x.shape[2:]
        width = s_gate.shape[1]
        dev, e = expert[0, 0] // OWN, expert[0, 0] % OWN
        place = (dev // 8) * 2 + dev % 2
        code = ((dev // 2) % 4) * 1024 + (e * PLANE + place) * SLOTS + slot[0, 0]
        code = jnp.where(slot[0, 0] < SLOTS, code, -1)
        tab = jnp.concatenate([code.T.astype(F32), gate[0, 0].T], axis=0)
        vmem = pl.BlockSpec(memory_space=pltpu.VMEM)
        hbm = pl.BlockSpec(memory_space=pl.ANY)
        dma = pltpu.SemaphoreType.DMA
        rows = PLANE * PAD
        y = pl.pallas_call(
            kernel,
            name="moe",
            out_shape=jax.ShapeDtypeStruct((tokens, depth), BF16),
            in_specs=[vmem, vmem] + [hbm] * 6,
            out_specs=vmem,
            scratch_shapes=[
                pltpu.VMEM((LINE - 1, tokens, depth), BF16),
                pltpu.VMEM((LINE - 1, 16, tokens), F32),
                pltpu.VMEM((LINE, OWN, PLANE, PAD, depth), BF16),
                pltpu.VMEM((LINE, OWN, PLANE, PAD, depth), BF16),
                pltpu.VMEM((LINE, OWN, PLANE, PAD, depth), BF16),
                pltpu.VMEM((LINE - 1, tokens, depth), BF16),
                pltpu.VMEM((tokens, depth), F32),
                pltpu.VMEM((rows, width), BF16),
                pltpu.VMEM((2, BLOCKS * PAD, tokens), BF16),
                pltpu.VMEM((BLOCKS * HALF, tokens), BF16),
                pltpu.VMEM((DEEP_F, 2, depth, WIDE), BF16),
                pltpu.VMEM((DEEP_D, width, COLS), BF16),
                dma((LINE - 1, 2)), dma((LINE - 1, 2)),
                dma((LINE, PLANE)), dma((LINE, PLANE)),
                dma((len(BACK), PLANE)), dma((len(BACK), PLANE)),
                dma((LINE - 1,)), dma((LINE - 1,)),
                dma((DEEP_F, 2)), dma((DEEP_D,)),
            ],
            compiler_params=pltpu.CompilerParams(
                collective_id=0, has_side_effects=True, vmem_limit_bytes=67043328
            ),
        )(x[0, 0], tab, w_gate, w_up, w_down, s_gate, s_up, s_down)
        return y[None, None]

    row = P("dp", "ep", None, None)
    w = P("ep", None, None)
    s = P(None, None)
    return jax.shard_map(
        step, mesh=mesh, in_specs=(row, row, row, row, w, w, w, s, s, s), out_specs=row, check_vma=False
    )
```

time: 709 us -> 261 us (0.37); the launches traced: 700 us -> 260 us
  waiting for transfers between devices: 426 us -> 0 us
  Pallas kernels: 0 us -> 256 us
  matrix products: 132 us -> 0 us
  local copies, waits for them, and re-layouts: 61.8 us -> 2.16 us
  blocking collectives: 46.6 us -> 0 us
  other arithmetic: 19.3 us -> 2.05 us
  between operations: 13.7 us -> 0.01 us
    reduce_scatter x1 -> x0, waiting for transfers between devices: 310 us -> none  [step(): y = lax.psum_scatter(part, 'ep', scatter_dimension=0, tiled=False)]
    pallas_call x0 -> x1, Pallas kernels: none -> 256 us  [step(): pl.pallas_call(kernel, name='moe', out_shape=jax.ShapeDtypeStruct((tokens...]
    dot_general x6 -> x0, matrix products: 132 us -> none  [dot(): return jnp.einsum(form, a, b, preferred_element_type=F32)]
    all_gather x1 -> x0, waiting for transfers between devices: 116 us -> none  [step(): xs = lax.all_gather(x0, 'ep')]
    all_gather x1 -> x0, blocking collectives: 46.6 us -> none  [step(): ts = lax.all_gather(table, 'ep')]
    transpose x2 -> x0, local copies, waits for them, and re-layouts: 25.6 us -> none  [the longest x1 12.9 us: step(): z.reshape(members, own, slots, -1).transpose(1, 0, 2, 3)]
    reshape x2 -> x0, local copies, waits for them, and re-layouts: 25.1 us -> none  [the longest x1 12.6 us: step(): out.reshape(own, members, slots, -1).transpose(1, 0, 2, 3)]
    convert_element_type x1 -> x0, local copies, waits for them, and re-layouts: 9.97 us -> none  [step(): z = dot('spt,std->spd', pick, xs).astype(BF16)]
  transfers between devices with their start and end apart: 2 -> 0, of which waited for: 2 -> 0; matrix products, arithmetic and copies ran while one was open for 3% -> 0% of each run, Pallas kernels for 0% -> 0%
where the time goes in v2:
time: 261 us; the launch traced here: 260 us
  Pallas kernels  256 us (98%)
    pallas_call x1, Pallas kernels, step(): pl.pallas_call(kernel, name='moe', out_shape=jax.ShapeDtypeStruct((tokens...  256 us

profile of v2, /device:TPU:0, one launch (start us, length us, event | category | flops | bytes accessed | tf_op | source)
XLA Modules:
  0.0 260.3 jit_solution(16117329498759384886)
XLA Ops:
  0.0 0.7 fusion.6
  0.8 1.3 pad_maximum_fusion.tab
  2.1 256.1 %moe.1 = bf16[256,1792]{1,0:T(8,128)(2,1)} custom-call(bf16[256,1792]{1,0:T(8,128)(2,1)} %bitcast.35, f32[16,256]{1,0:T(8,128)} %pad_maximum_fusion.tab, bf16[3,1792,2048]{2,1,0:T(8,128)(2,1)} %w_gate.1, bf16[3,1792,2048]{2,1,0:T(8,128)(2,1)} %w_up.1, bf16[3,2048,1792]{2,1,0:T(8,128)(2,1)} %w_down.1, bf16[1792,2048]{1,0:T(8,128)(2,1)} %s_gate.1, ...), custom_call_target="tpu_custom_call" | custom-call | tf_op jit(solution)/shard_map/moe/pallas_call | solution.py:307
  258.2 2.2 copy.12
